TPU v7x, 32 devices: a whole 2x2x4 slice. The times are simulated.
32 devices in a mesh: section: 4 (over y, x), tok: 8 (over z, core).
Axes of the slice: x: 2, y: 2, z: 4, core: 2. Of those that a mesh axis runs over, the one named last changes fastest.
Arguments:
- activations: bfloat16 [8, 2048, 8192], P('section', 'tok'), may hold values from -12 to 12
- projection: bfloat16 [8192, 512], P('tok'), may hold values from -0.0625 to 0.0625
Outputs:
- sketch: float32 [8, 512, 512], P('section', None, 'tok')
- similarity: float32 [8, 2], P('section')
All inputs are finite; a program needn't handle non-finite values.
Results may differ from a plain program's by a relative error of at most 0.0003.
Values may be sent and summed in bfloat16 or wider, within the bound.
A program may use at most 64 MiB of HBM per device.

v0:
```python
import jax
import jax.numpy as jnp
from jax import lax
from jax.sharding import PartitionSpec as P


def shifted(block, axis, distance):
    devices = range(lax.axis_size(axis))
    route = [(i - distance, i) for i in devices if i - distance in devices]
    return lax.ppermute(block, axis, route)


def frobenius(first, second):
    return jnp.sum(first * second, axis=(-2, -1))


def local_products(local_sketch, prev_last, next_first, section_index, sections):
    before = jnp.where(section_index == 0, local_sketch[0], prev_last)
    beyond = jnp.where(section_index == sections - 1, local_sketch[-1], next_first)
    squares = frobenius(local_sketch, local_sketch)
    chained = frobenius(local_sketch[:-1], local_sketch[1:])
    edges = jnp.stack(
        [
            frobenius(before, local_sketch[0]),
            frobenius(local_sketch[-1], beyond),
            frobenius(before, before),
            frobenius(beyond, beyond),
        ]
    )
    return jnp.concatenate([squares, chained, edges])


def finish(products, layers):
    squares = products[:layers]
    chained = products[layers : 2 * layers - 1]
    edges = products[2 * layers - 1 :]
    ext_squares = jnp.concatenate([edges[2:3], squares, edges[3:4]])
    ext_chained = jnp.concatenate([edges[0:1], chained, edges[1:2]])
    ratios = ext_chained / jnp.sqrt(ext_squares[:-1] * ext_squares[1:])
    return jnp.stack([ratios[:-1], ratios[1:]], axis=1)


def local(activations, projection):
    layers, tok_rows, model_width = activations.shape
    sketch_width = projection.shape[1]
    groups = lax.axis_size("tok")
    total_tokens = tok_rows * groups
    flat_acts = activations.reshape(layers * tok_rows, model_width)
    projected = jnp.dot(
        flat_acts,
        lax.all_gather(projection, "tok", axis=0, tiled=True),
        preferred_element_type=jnp.float32,
    )
    projected = projected.reshape(layers, tok_rows, sketch_width)
    raw_gram = jnp.einsum("ltr,lts->lrs", projected, projected, precision=lax.Precision.HIGHEST)
    local_sums = jnp.sum(projected, axis=1)
    tok_index = lax.axis_index("tok")
    section_index = lax.axis_index("section")
    sections = lax.axis_size("section")
    columns_dev = sketch_width // groups
    shares = lax.psum_scatter(raw_gram, "tok", scatter_dimension=2, tiled=True)
    totals = lax.psum(local_sums, "tok")
    local_totals = lax.dynamic_slice_in_dim(totals, tok_index * columns_dev, columns_dev, 1)
    local_sketch = shares - totals[:, :, None] * local_totals[:, None, :] / total_tokens
    next_first = shifted(local_sketch[0].astype(jnp.bfloat16), "section", -1).astype(jnp.float32)
    prev_last = shifted(local_sketch[layers - 1].astype(jnp.bfloat16), "section", 1).astype(
        jnp.float32
    )
    partial_products = local_products(local_sketch, prev_last, next_first, section_index, sections)
    products = lax.psum(partial_products, "tok")
    return (local_sketch, finish(products, layers))


def solution(mesh):
    return jax.shard_map(
        local,
        mesh=mesh,
        in_specs=(P("section", "tok", None), P("tok", None)),
        out_specs=(P("section", None, "tok"), P("section", None)),
        check_vma=False,
    )
```

profile of v0, /device:TPU:5, one launch (start us, length us, event | category | flops | bytes accessed | tf_op | source)
XLA Modules:
  0.0 181.1 jit_solution(8922740263490484385)
XLA Ops:
  7.2 0.0 all-gather.2.cloned.1.call-start
  7.2 0.7 all-gather.2.cloned.1.call-update
  7.9 0.0 reduce-scatter.2.cloned.1.call-start
  7.9 85.3 %all-gather.2.cloned.1.call-done = bf16[8192,512]{1,0:T(8,128)(2,1)} async-done(((bf16[1024,512]{1,0:T(8,128)(2,1)}), bf16[8192,512]{1,0:T(8,128)(2,1)}) %all-gather.2.cloned.1.call-update) | async-done | bytes 8388624 | tf_op jit(solution)/shard_map/all_gather | solution.py:51
  93.2 9.5 %fusion.6 = (f32[2,512]{1,0:T(2,128)S(1)}, f32[2,256,512]{2,1,0:T(8,128)S(1)}) fusion(bf16[2,256,8192]{2,1,0:T(8,128)(2,1)} %param.2, bf16[8192,512]{1,0:T(8,128)(2,1)} %all-gather.2.cloned.1.call-done), kind=kOutput, calls=%fused_computation.23 | convolution fusion | flops 4295228416 | bytes 17829888 | tf_op jit(solution)/shard_map/dot_general | solution.py:49
  102.7 3.3 %fusion.7 = f32[2,512,512]{1,2,0:T(8,128)} fusion(f32[2,256,512]{2,1,0:T(8,128)S(1)} %get-tuple-element.22), kind=kOutput, calls=%fused_computation.24 | convolution fusion | flops 1610612736 | bytes 3145728 | tf_op jit(solution)/shard_map/ltr,lts->lrs/dot_general | solution.py:55
  106.0 0.0 reduce-scatter.2.cloned.1.call-update
  106.1 13.5 %psum.14 = f32[2,512]{1,0:T(2,128)S(1)} all-reduce(f32[2,512]{1,0:T(2,128)S(1)} %get-tuple-element.21), channel_id=1, replica_groups=mesh['section'=4,'tok'=8] {'tok'}, use_global_device_ids=true, to_apply=%region_2.0 | all-reduce | flops 1024 | bytes 8192 | tf_op jit(solution)/shard_map/psum | solution.py:62
  119.6 0.1 constant_dynamic-slice_fusion
  119.7 18.1 %reduce-scatter.2.cloned.1.call-done = f32[2,512,64]{1,2,0:T(8,128)} async-done(((f32[2,512,512]{1,2,0:T(8,128)}), f32[2,512,64]{1,2,0:T(8,128)}) %reduce-scatter.2.cloned.1.call-update) | async-done | bytes 262160 | tf_op jit(solution)/shard_map/reduce_scatter | solution.py:61
  137.7 1.2 multiply_reduce_fusion
  138.9 0.0 copy-start
  138.9 3.1 %collective-permute-start.1 = (bf16[512,64]{0,1:T(8,128)(2,1)S(1)}, bf16[512,64]{0,1:T(8,128)(2,1)S(1)}, u32[]{:S(2)}, u32[]{:S(2)}) collective-permute-start(bf16[512,64]{0,1:T(8,128)(2,1)S(1)} %get-tuple-element.13), channel_id=1, source_target_pairs={{8,0},{16,8},{24,16},{9,1},{17,9},{25,17},{10,2},{18,10},{26,18},{... | collective-permute-start | bytes 196616 | tf_op jit(solution)/shard_map/ppermute | solution.py:10
  142.0 2.2 %collective-permute-start = (bf16[512,64]{0,1:T(8,128)(2,1)S(1)}, bf16[512,64]{0,1:T(8,128)(2,1)S(1)}, u32[]{:S(2)}, u32[]{:S(2)}) collective-permute-start(bf16[512,64]{0,1:T(8,128)(2,1)S(1)} %get-tuple-element.12), channel_id=1, source_target_pairs={{0,8},{8,16},{16,24},{1,9},{9,17},{17,25},{2,10},{10,18},{18,26},{... | collective-permute-start | bytes 196616 | tf_op jit(solution)/shard_map/ppermute | solution.py:10
  144.2 0.6 multiply_reduce_fusion.3
  144.8 0.0 collective-permute-done.1
  144.8 3.6 %collective-permute-done = bf16[512,64]{0,1:T(8,128)(2,1)S(1)} collective-permute-done((bf16[512,64]{0,1:T(8,128)(2,1)S(1)}, bf16[512,64]{0,1:T(8,128)(2,1)S(1)}, u32[]{:S(2)}, u32[]{:S(2)}) %collective-permute-start) | collective-permute-done | bytes 65568 | tf_op jit(solution)/shard_map/ppermute | solution.py:10
  148.4 0.7 multiply_reduce_fusion.1
  149.2 3.2 %concatenate.13 = f32[7]{0:T(128)S(1)} concatenate(f32[2]{0:T(128)S(1)} %get-tuple-element.10, f32[1]{0:T(128)} %bitcast.1, f32[1]{0:T(128)} %bitcast.4, f32[1]{0:T(128)} %bitcast.5, f32[1]{0:T(128)} %bitcast.6, f32[1]{0:T(128)} %bitcast.7), dimensions={0} | concatenate | bytes 56 | tf_op jit(solution)/shard_map/concatenate | solution.py:30
  152.4 17.2 %psum.15 = f32[7]{0:T(128)S(1)} all-reduce(f32[7]{0:T(128)S(1)} %concatenate.13), channel_id=1, replica_groups=mesh['section'=4,'tok'=8] {'tok'}, use_global_device_ids=true, to_apply=%region_9.10 | all-reduce | flops 7 | bytes 56 | tf_op jit(solution)/shard_map/psum | solution.py:70
  169.6 0.7 fusion.5
  170.2 3.2 %maximum_multiply_fusion = f32[3]{0:T(128)S(1)} fusion(f32[1]{0:T(128)} %get-tuple-element.18, f32[1]{0:T(128)} %get-tuple-element.19, f32[1]{0:T(128)} %get-tuple-element.20, f32[2]{0:T(128)S(1)} %bitcast.38, f32[1]{0:T(128)} %get-tuple-element.17, f32[1]{0:T(128)} %get-tuple-element.16), kind=kLoop, calls=%fused_computation.16 | loop fusion | flops 18 | bytes 40 | tf_op jit(solution)/shard_map/div | solution.py:39
  173.5 0.1 slice_bitcast_fusion.1
  173.6 0.7 copy.5
  174.2 0.0 copy-done
  (2 shorter events, 0.0 us)
Async XLA Ops:
  7.2 86.1 %all-gather.2.cloned.1.call-start = ((), (), s32[]{:S(2)}) async-start(), calls=%async_computation.1 | async-start | bytes 9437184 | tf_op jit(solution)/shard_map/all_gather | solution.py:51
  7.9 129.8 %reduce-scatter.2.cloned.1.call-start = ((), (), s32[]{:S(2)}) async-start(), calls=%async_computation.2 | async-start | bytes 2359296 | tf_op jit(solution)/shard_map/reduce_scatter | solution.py:61
  138.9 35.3 %copy-start = (f32[2,512,64]{1,2,0:T(8,128)}, f32[2,512,64]{1,2,0:T(8,128)S(1)}, u32[]{:S(2)}) copy-start(f32[2,512,64]{1,2,0:T(8,128)S(1)} %get-tuple-element.11) | copy-start | bytes 786436
  138.9 5.9 %collective-permute-start.1 = (bf16[512,64]{0,1:T(8,128)(2,1)S(1)}, bf16[512,64]{0,1:T(8,128)(2,1)S(1)}, u32[]{:S(2)}, u32[]{:S(2)}) collective-permute-start(bf16[512,64]{0,1:T(8,128)(2,1)S(1)} %get-tuple-element.13), channel_id=1, source_target_pairs={{8,0},{16,8},{24,16},{9,1},{17,9},{25,17},{10,2},{18,10},{26,18},{... | collective-permute-start | bytes 196616 | tf_op jit(solution)/shard_map/ppermute | solution.py:10
  142.0 6.4 %collective-permute-start = (bf16[512,64]{0,1:T(8,128)(2,1)S(1)}, bf16[512,64]{0,1:T(8,128)(2,1)S(1)}, u32[]{:S(2)}, u32[]{:S(2)}) collective-permute-start(bf16[512,64]{0,1:T(8,128)(2,1)S(1)} %get-tuple-element.12), channel_id=1, source_target_pairs={{0,8},{8,16},{16,24},{1,9},{9,17},{17,25},{2,10},{10,18},{18,26},{... | collective-permute-start | bytes 196616 | tf_op jit(solution)/shard_map/ppermute | solution.py:10
Sparse Core Ops, SparseCore 0:
  9.6 83.6 all-gather.1
  106.2 31.4 reduce-scatter.1
where the time goes:
time: 181 us
  waiting for transfers between devices  108 us (60%)
  blocking collectives  30.7 us (17%)
  between operations  14.1 us (8%)
  matrix products  12.8 us (7%)
  other arithmetic  5.78 us (3%)
  starting transfers between devices  5.36 us (3%)
  local copies, waits for them, and re-layouts  4.73 us (3%)
    all_gather x1, waiting for transfers between devices, local(): lax.all_gather(projection, 'tok', axis=0, tiled=True)  85.3 us
    reduce_scatter x1, waiting for transfers between devices, local(): shares = lax.psum_scatter(raw_gram, 'tok', scatter_dimension=2, tiled=True)  18.1 us
    psum x1, blocking collectives, local(): products = lax.psum(partial_products, 'tok')  17.2 us
    psum x1, blocking collectives, local(): totals = lax.psum(local_sums, 'tok')  13.5 us
    dot_general x1, matrix products, local(): jnp.dot(flat_acts, lax.all_gather(projection, 'tok', axis=0, tiled=True),...  9.49 us
    ppermute x2, starting transfers between devices, shifted(): return lax.ppermute(block, axis, route)  5.28 us
  transfers between devices with their start and end apart: 4, of which 3 were waited for; matrix products, arithmetic and copies ran while one was open for 0% of the time, Pallas kernels for 0%

commit v1 on v0

--- a/solution.py
+++ b/solution.py
@@ -1,7 +1,16 @@
+import functools
 import jax
 import jax.numpy as jnp
 from jax import lax
 from jax.sharding import PartitionSpec as P
+from jax.lax import all_gather
+
+
+def mix_the_series_all(panel, link_axis):
+    return jnp.sum(all_gather(panel, axis_name=link_axis), 0)
+
+
+remake_knots = functools.partial(mix_the_series_all, link_axis="tok")
 
 
 def shifted(block, axis, distance):
@@ -67,7 +76,7 @@
         jnp.float32
     )
     partial_products = local_products(local_sketch, prev_last, next_first, section_index, sections)
-    products = lax.psum(partial_products, "tok")
+    products = remake_knots(partial_products)
     return (local_sketch, finish(products, layers))
 
 

time: 181 us -> 182 us (level)
  waiting for transfers between devices: 108 us -> 106 us
    unnamed x0 -> x1, blocking collectives: none -> 17.2 us
    psum x1 -> x0, blocking collectives: 17.2 us -> none  [local(): products = lax.psum(partial_products, 'tok')]
  transfers between devices with their start and end apart: 4 -> 4, of which waited for: 3 -> 3; matrix products, arithmetic and copies ran while one was open for 0% -> 1% of each run, Pallas kernels for 0% -> 0%
where the time goes in v1:
time: 182 us
  waiting for transfers between devices  106 us (58%)
  blocking collectives  30.9 us (17%)
  between operations  14.8 us (8%)
  matrix products  12.8 us (7%)
  other arithmetic  5.81 us (3%)
  local copies, waits for them, and re-layouts  5.61 us (3%)
  starting transfers between devices  5.36 us (3%)
    all_gather x1, waiting for transfers between devices, local(): lax.all_gather(projection, 'tok', axis=0, tiled=True)  85.3 us
    unnamed x1, blocking collectives  17.2 us
    reduce_scatter x1, waiting for transfers between devices, local(): shares = lax.psum_scatter(raw_gram, 'tok', scatter_dimension=2, tiled=True)  16.7 us
    psum x1, blocking collectives, local(): totals = lax.psum(local_sums, 'tok')  13.6 us
    dot_general x1, matrix products, local(): jnp.dot(flat_acts, lax.all_gather(projection, 'tok', axis=0, tiled=True),...  9.49 us
    ppermute x2, starting transfers between devices, shifted(): return lax.ppermute(block, axis, route)  5.28 us
    ppermute x2, waiting for transfers between devices, shifted(): return lax.ppermute(block, axis, route)  3.76 us
  transfers between devices with their start and end apart: 4, of which 3 were waited for; matrix products, arithmetic and copies ran while one was open for 1% of the time, Pallas kernels for 0%

profile of v1, /device:TPU:5, one launch (start us, length us, event | category | flops | bytes accessed | tf_op | source)
XLA Modules:
  0.0 181.7 jit_solution(6030657810617556170)
XLA Ops:
  7.2 0.0 all-gather.3.cloned.1.call-start
  7.2 0.7 all-gather.3.cloned.1.call-update
  7.9 0.0 copy-start.1
  7.9 0.0 reduce-scatter.2.cloned.1.call-start
  8.0 85.3 %all-gather.3.cloned.1.call-done = bf16[8192,512]{1,0:T(8,128)(2,1)} async-done(((bf16[1024,512]{1,0:T(8,128)(2,1)}), bf16[8192,512]{1,0:T(8,128)(2,1)}) %all-gather.3.cloned.1.call-update) | async-done | bytes 8388624 | tf_op jit(solution)/shard_map/all_gather | solution.py:60
  93.2 9.5 %fusion.6 = (f32[2,512]{1,0:T(2,128)S(1)}, f32[2,256,512]{2,1,0:T(8,128)S(1)}) fusion(bf16[2,256,8192]{2,1,0:T(8,128)(2,1)} %param.2, bf16[8192,512]{1,0:T(8,128)(2,1)} %all-gather.3.cloned.1.call-done), kind=kOutput, calls=%fused_computation.23 | convolution fusion | flops 4295228416 | bytes 17829888 | tf_op jit(solution)/shard_map/dot_general | solution.py:58
  102.7 3.3 %fusion.7 = f32[2,512,512]{1,2,0:T(8,128)} fusion(f32[2,256,512]{2,1,0:T(8,128)S(1)} %get-tuple-element.22), kind=kOutput, calls=%fused_computation.24 | convolution fusion | flops 1610612736 | bytes 3145728 | tf_op jit(solution)/shard_map/ltr,lts->lrs/dot_general | solution.py:64
  106.0 0.0 reduce-scatter.2.cloned.1.call-update
  106.1 0.0 copy-done.1
  106.1 0.6 dynamic-slice
  107.3 13.6 %psum.7 = f32[2,512]{1,0:T(2,128)S(1)} all-reduce(f32[2,512]{1,0:T(2,128)S(1)} %get-tuple-element.21), channel_id=1, replica_groups=mesh['section'=4,'tok'=8] {'tok'}, use_global_device_ids=true, to_apply=%region_2.0 | all-reduce | flops 1024 | bytes 8192 | tf_op jit(solution)/shard_map/psum | solution.py:71
  121.0 0.1 constant_dynamic-slice_fusion
  121.0 16.7 %reduce-scatter.2.cloned.1.call-done = f32[2,512,64]{1,2,0:T(8,128)} async-done(((f32[2,512,512]{1,2,0:T(8,128)}), f32[2,512,64]{1,2,0:T(8,128)}) %reduce-scatter.2.cloned.1.call-update) | async-done | bytes 262160 | tf_op jit(solution)/shard_map/reduce_scatter | solution.py:70
  137.8 1.2 multiply_reduce_fusion
  138.9 0.0 copy-start
  139.0 3.1 %collective-permute-start.1 = (bf16[512,64]{0,1:T(8,128)(2,1)S(1)}, bf16[512,64]{0,1:T(8,128)(2,1)S(1)}, u32[]{:S(2)}, u32[]{:S(2)}) collective-permute-start(bf16[512,64]{0,1:T(8,128)(2,1)S(1)} %get-tuple-element.13), channel_id=1, source_target_pairs={{8,0},{16,8},{24,16},{9,1},{17,9},{25,17},{10,2},{18,10},{26,18},{... | collective-permute-start | bytes 196616 | tf_op jit(solution)/shard_map/ppermute | solution.py:19
  142.1 2.2 %collective-permute-start = (bf16[512,64]{0,1:T(8,128)(2,1)S(1)}, bf16[512,64]{0,1:T(8,128)(2,1)S(1)}, u32[]{:S(2)}, u32[]{:S(2)}) collective-permute-start(bf16[512,64]{0,1:T(8,128)(2,1)S(1)} %get-tuple-element.12), channel_id=1, source_target_pairs={{0,8},{8,16},{16,24},{1,9},{9,17},{17,25},{2,10},{10,18},{18,26},{... | collective-permute-start | bytes 196616 | tf_op jit(solution)/shard_map/ppermute | solution.py:19
  144.3 0.6 multiply_reduce_fusion.3
  144.9 0.0 collective-permute-done.1
  144.9 3.8 %collective-permute-done = bf16[512,64]{0,1:T(8,128)(2,1)S(1)} collective-permute-done((bf16[512,64]{0,1:T(8,128)(2,1)S(1)}, bf16[512,64]{0,1:T(8,128)(2,1)S(1)}, u32[]{:S(2)}, u32[]{:S(2)}) %collective-permute-start) | collective-permute-done | bytes 65568 | tf_op jit(solution)/shard_map/ppermute | solution.py:19
  148.7 0.7 multiply_reduce_fusion.1
  149.4 3.2 %concatenate.13 = f32[7]{0:T(128)S(1)} concatenate(f32[2]{0:T(128)S(1)} %get-tuple-element.10, f32[1]{0:T(128)} %bitcast.1, f32[1]{0:T(128)} %bitcast.4, f32[1]{0:T(128)} %bitcast.5, f32[1]{0:T(128)} %bitcast.6, f32[1]{0:T(128)} %bitcast.7), dimensions={0} | concatenate | bytes 56 | tf_op jit(solution)/shard_map/concatenate | solution.py:39
  152.6 0.2 dynamic-update-slice
  152.8 17.2 %all-reduce = f32[56]{0:T(128)S(1)} all-reduce(f32[56]{0:T(128)S(1)} %dynamic-update-slice), channel_id=2, replica_groups=mesh['section'=4,'tok'=8] {'tok'}, use_global_device_ids=true, to_apply=%add | all-reduce | flops 56 | bytes 448
  170.1 0.1 reshape.11
  170.2 0.7 fusion.5
  170.9 3.2 %maximum_multiply_fusion = f32[3]{0:T(128)S(1)} fusion(f32[1]{0:T(128)} %get-tuple-element.18, f32[1]{0:T(128)} %get-tuple-element.19, f32[1]{0:T(128)} %get-tuple-element.20, f32[2]{0:T(128)S(1)} %bitcast.39, f32[1]{0:T(128)} %get-tuple-element.17, f32[1]{0:T(128)} %get-tuple-element.16), kind=kLoop, calls=%fused_computation.16 | loop fusion | flops 18 | bytes 40 | tf_op jit(solution)/shard_map/div | solution.py:48
  174.1 0.1 slice_bitcast_fusion.1
  174.2 0.7 copy.5
  174.8 0.0 copy-done
  (4 shorter events, 0.1 us)
Async XLA Ops:
  7.2 86.1 %all-gather.3.cloned.1.call-start = ((), (), s32[]{:S(2)}) async-start(), calls=%async_computation.1 | async-start | bytes 9437184 | tf_op jit(solution)/shard_map/all_gather | solution.py:60
  7.9 98.2 %copy-start.1 = (u32[32]{0:T(128)S(1)}, u32[32]{0:T(128)}, u32[]{:S(2)}) copy-start(u32[32]{0:T(128)} %constant.24) | copy-start | bytes 388
  7.9 129.9 %reduce-scatter.2.cloned.1.call-start = ((), (), s32[]{:S(2)}) async-start(), calls=%async_computation.2 | async-start | bytes 2359296 | tf_op jit(solution)/shard_map/reduce_scatter | solution.py:70
  138.9 35.9 %copy-start = (f32[2,512,64]{1,2,0:T(8,128)}, f32[2,512,64]{1,2,0:T(8,128)S(1)}, u32[]{:S(2)}) copy-start(f32[2,512,64]{1,2,0:T(8,128)S(1)} %get-tuple-element.11) | copy-start | bytes 786436
  139.0 5.9 %collective-permute-start.1 = (bf16[512,64]{0,1:T(8,128)(2,1)S(1)}, bf16[512,64]{0,1:T(8,128)(2,1)S(1)}, u32[]{:S(2)}, u32[]{:S(2)}) collective-permute-start(bf16[512,64]{0,1:T(8,128)(2,1)S(1)} %get-tuple-element.13), channel_id=1, source_target_pairs={{8,0},{16,8},{24,16},{9,1},{17,9},{25,17},{10,2},{18,10},{26,18},{... | collective-permute-start | bytes 196616 | tf_op jit(solution)/shard_map/ppermute | solution.py:19
  142.1 6.6 %collective-permute-start = (bf16[512,64]{0,1:T(8,128)(2,1)S(1)}, bf16[512,64]{0,1:T(8,128)(2,1)S(1)}, u32[]{:S(2)}, u32[]{:S(2)}) collective-permute-start(bf16[512,64]{0,1:T(8,128)(2,1)S(1)} %get-tuple-element.12), channel_id=1, source_target_pairs={{0,8},{8,16},{16,24},{1,9},{9,17},{17,25},{2,10},{10,18},{18,26},{... | collective-permute-start | bytes 196616 | tf_op jit(solution)/shard_map/ppermute | solution.py:19
Sparse Core Ops, SparseCore 0:
  9.6 83.6 all-gather.2
  106.2 31.5 reduce-scatter.1

commit v2 on v0

--- a/solution.py
+++ b/solution.py
@@ -2,6 +2,13 @@
 import jax.numpy as jnp
 from jax import lax
 from jax.sharding import PartitionSpec as P
+
+
+def space_switch(local_x, axis_name, dim_i):
+    arr_now = lax.axis_size(axis_name)
+    y_new = jnp.stack([local_x] * arr_now)
+    local_next = lax.all_to_all(y_new, axis_name=axis_name, split_axis=0, concat_axis=0)
+    return jnp.concatenate(local_next, axis=dim_i)
 
 
 def shifted(block, axis, distance):
@@ -47,9 +54,7 @@
     total_tokens = tok_rows * groups
     flat_acts = activations.reshape(layers * tok_rows, model_width)
     projected = jnp.dot(
-        flat_acts,
-        lax.all_gather(projection, "tok", axis=0, tiled=True),
-        preferred_element_type=jnp.float32,
+        flat_acts, space_switch(projection, "tok", 0), preferred_element_type=jnp.float32
     )
     projected = projected.reshape(layers, tok_rows, sketch_width)
     raw_gram = jnp.einsum("ltr,lts->lrs", projected, projected, precision=lax.Precision.HIGHEST)

time: 181 us -> 285 us (1.57)
  blocking collectives: 30.7 us -> 220 us
  waiting for transfers between devices: 108 us -> 22.1 us
    all_to_all x0 -> x1, blocking collectives: none -> 188 us  [space_switch(): lax.all_to_all(y_new, axis_name=axis_name, split_axis=0, concat_axis=0)]
    all_gather x1 -> x0, waiting for transfers between devices: 85.3 us -> none  [local(): lax.all_gather(projection, 'tok', axis=0, tiled=True)]
  transfers between devices with their start and end apart: 4 -> 3, of which waited for: 3 -> 2; matrix products, arithmetic and copies ran while one was open for 0% -> 0% of each run, Pallas kernels for 0% -> 0%
where the time goes in v2:
time: 285 us; the launch traced here: 284 us
  blocking collectives  220 us (77%)
  waiting for transfers between devices  22.1 us (8%)
  between operations  14.1 us (5%)
  matrix products  10.4 us (4%)
  local copies, waits for them, and re-layouts  6.69 us (2%)
  other arithmetic  5.78 us (2%)
  starting transfers between devices  5.32 us (2%)
    all_to_all x1, blocking collectives, space_switch(): lax.all_to_all(y_new, axis_name=axis_name, split_axis=0, concat_axis=0)  188 us
    reduce_scatter x1, waiting for transfers between devices, local(): shares = lax.psum_scatter(raw_gram, 'tok', scatter_dimension=2, tiled=True)  18.3 us
    psum x1, blocking collectives, local(): products = lax.psum(partial_products, 'tok')  17.4 us
    psum x1, blocking collectives, local(): totals = lax.psum(local_sums, 'tok')  14.3 us
    dot_general x1, matrix products, local(): jnp.dot(flat_acts, space_switch(projection, 'tok', 0), preferred_element_...  7.11 us
  transfers between devices with their start and end apart: 3, of which 2 were waited for; matrix products, arithmetic and copies ran while one was open for 0% of the time, Pallas kernels for 0%

profile of v2, /device:TPU:5, one launch (start us, length us, event | category | flops | bytes accessed | tf_op | source)
XLA Modules:
  0.0 284.3 jit_solution(14092672945231971822)
XLA Ops:
  7.2 0.0 reduce-scatter.2.cloned.1.call-start
  7.2 2.0 stack.32
  9.2 188.2 %all_to_all.5 = bf16[8,1024,512]{2,1,0:T(8,128)(2,1)S(1)} all-to-all(bf16[8,1024,512]{2,1,0:T(8,128)(2,1)S(1)} %stack.32), channel_id=1, replica_groups=mesh['section'=4,'tok'=8] {'tok'}, dimensions={0} | all-to-all | bytes 16777216 | tf_op jit(solution)/shard_map/all_to_all | solution.py:10
  197.3 7.1 %fusion.4 = (f32[2,512]{1,0:T(2,128)S(1)}, f32[2,256,512]{2,1,0:T(8,128)S(1)}) fusion(bf16[2,256,8192]{2,1,0:T(8,128)(2,1)} %param.2, bf16[8192,512,1]{1,0,2:T(8,128)(2,1)S(1)} %bitcast.37), kind=kOutput, calls=%fused_computation.21 | convolution fusion | flops 4295228416 | bytes 17829888 | tf_op jit(solution)/shard_map/dot_general | solution.py:56
  204.5 3.3 %fusion.5 = f32[2,512,512]{1,2,0:T(8,128)} fusion(f32[2,256,512]{2,1,0:T(8,128)S(1)} %get-tuple-element.22), kind=kOutput, calls=%fused_computation.22 | convolution fusion | flops 1610612736 | bytes 3145728 | tf_op jit(solution)/shard_map/ltr,lts->lrs/dot_general | solution.py:60
  207.8 0.0 reduce-scatter.2.cloned.1.call-update
  207.8 14.3 %psum.14 = f32[2,512]{1,0:T(2,128)S(1)} all-reduce(f32[2,512]{1,0:T(2,128)S(1)} %get-tuple-element.21), channel_id=1, replica_groups=mesh['section'=4,'tok'=8] {'tok'}, use_global_device_ids=true, to_apply=%region_2.0 | all-reduce | flops 1024 | bytes 8192 | tf_op jit(solution)/shard_map/psum | solution.py:67
  222.1 0.1 constant_dynamic-slice_fusion
  222.2 18.3 %reduce-scatter.2.cloned.1.call-done = f32[2,512,64]{1,2,0:T(8,128)} async-done(((f32[2,512,512]{1,2,0:T(8,128)}), f32[2,512,64]{1,2,0:T(8,128)}) %reduce-scatter.2.cloned.1.call-update) | async-done | bytes 262160 | tf_op jit(solution)/shard_map/reduce_scatter | solution.py:66
  240.5 1.2 multiply_reduce_fusion
  241.7 0.0 copy-start
  241.7 3.1 %collective-permute-start.1 = (bf16[512,64]{0,1:T(8,128)(2,1)S(1)}, bf16[512,64]{0,1:T(8,128)(2,1)S(1)}, u32[]{:S(2)}, u32[]{:S(2)}) collective-permute-start(bf16[512,64]{0,1:T(8,128)(2,1)S(1)} %get-tuple-element.13), channel_id=1, source_target_pairs={{8,0},{16,8},{24,16},{9,1},{17,9},{25,17},{10,2},{18,10},{26,18},{... | collective-permute-start | bytes 196616 | tf_op jit(solution)/shard_map/ppermute | solution.py:17
  244.8 2.2 collective-permute-start
  247.0 0.6 multiply_reduce_fusion.3
  247.6 0.0 collective-permute-done.1
  247.6 3.7 %collective-permute-done = bf16[512,64]{0,1:T(8,128)(2,1)S(1)} collective-permute-done((bf16[512,64]{0,1:T(8,128)(2,1)S(1)}, bf16[512,64]{0,1:T(8,128)(2,1)S(1)}, u32[]{:S(2)}, u32[]{:S(2)}) %collective-permute-start) | collective-permute-done | bytes 65568 | tf_op jit(solution)/shard_map/ppermute | solution.py:17
  251.3 0.7 multiply_reduce_fusion.1
  252.1 3.2 %concatenate.13 = f32[7]{0:T(128)S(1)} concatenate(f32[2]{0:T(128)S(1)} %get-tuple-element.10, f32[1]{0:T(128)} %bitcast.2, f32[1]{0:T(128)} %bitcast.5, f32[1]{0:T(128)} %bitcast.6, f32[1]{0:T(128)} %bitcast.7, f32[1]{0:T(128)} %bitcast.8), dimensions={0} | concatenate | bytes 56 | tf_op jit(solution)/shard_map/concatenate | solution.py:37
  255.3 17.4 %psum.15 = f32[7]{0:T(128)S(1)} all-reduce(f32[7]{0:T(128)S(1)} %concatenate.13), channel_id=1, replica_groups=mesh['section'=4,'tok'=8] {'tok'}, use_global_device_ids=true, to_apply=%region_9.10 | all-reduce | flops 7 | bytes 56 | tf_op jit(solution)/shard_map/psum | solution.py:75
  272.8 0.7 fusion.3
  273.4 3.2 %maximum_multiply_fusion = f32[3]{0:T(128)S(1)} fusion(f32[1]{0:T(128)} %get-tuple-element.18, f32[1]{0:T(128)} %get-tuple-element.19, f32[1]{0:T(128)} %get-tuple-element.20, f32[2]{0:T(128)S(1)} %bitcast.38, f32[1]{0:T(128)} %get-tuple-element.17, f32[1]{0:T(128)} %get-tuple-element.16), kind=kLoop, calls=%fused_computation.14 | loop fusion | flops 18 | bytes 40 | tf_op jit(solution)/shard_map/div | solution.py:46
  276.7 0.1 slice_bitcast_fusion.1
  276.7 0.7 copy.5
  277.4 0.0 copy-done
  (2 shorter events, 0.0 us)
Async XLA Ops:
  7.2 233.3 %reduce-scatter.2.cloned.1.call-start = ((), (), s32[]{:S(2)}) async-start(), calls=%async_computation.2 | async-start | bytes 2359296 | tf_op jit(solution)/shard_map/reduce_scatter | solution.py:66
  241.7 35.8 %copy-start = (f32[2,512,64]{1,2,0:T(8,128)}, f32[2,512,64]{1,2,0:T(8,128)S(1)}, u32[]{:S(2)}) copy-start(f32[2,512,64]{1,2,0:T(8,128)S(1)} %get-tuple-element.11) | copy-start | bytes 786436
  241.7 5.9 %collective-permute-start.1 = (bf16[512,64]{0,1:T(8,128)(2,1)S(1)}, bf16[512,64]{0,1:T(8,128)(2,1)S(1)}, u32[]{:S(2)}, u32[]{:S(2)}) collective-permute-start(bf16[512,64]{0,1:T(8,128)(2,1)S(1)} %get-tuple-element.13), channel_id=1, source_target_pairs={{8,0},{16,8},{24,16},{9,1},{17,9},{25,17},{10,2},{18,10},{26,18},{... | collective-permute-start | bytes 196616 | tf_op jit(solution)/shard_map/ppermute | solution.py:17
  244.8 6.5 %collective-permute-start = (bf16[512,64]{0,1:T(8,128)(2,1)S(1)}, bf16[512,64]{0,1:T(8,128)(2,1)S(1)}, u32[]{:S(2)}, u32[]{:S(2)}) collective-permute-start(bf16[512,64]{0,1:T(8,128)(2,1)S(1)} %get-tuple-element.12), channel_id=1, source_target_pairs={{0,8},{8,16},{16,24},{1,9},{9,17},{17,25},{2,10},{10,18},{18,26},{... | collective-permute-start | bytes 196616 | tf_op jit(solution)/shard_map/ppermute | solution.py:17
Sparse Core Ops, SparseCore 0:
  207.9 32.5 reduce-scatter.1
